TPU v7x, 512 devices: a whole 4x4x16 slice. The times are simulated.
512 devices in a mesh: tm: 32 (over y, x, core), diag: 16 (over z).
Axes of the slice: x: 4, y: 4, z: 16, core: 2. Of those that a mesh axis runs over, the one named last changes fastest.
Arguments:
- series: float32 [524288], P('tm'), may hold values from -6 to 6
- tail: float32 [256], replicated, may hold values from -6 to 6
- diag_offsets: int32 [16], P('diag'), may hold values from 0 to 12000, as said below
- exclusion: int32 [1], replicated, may hold values from 64 to 255
Outputs:
- profile: float32 [524288], P(('tm', 'diag'))
Inputs may be any that keep to these rules, and one draw needn't show every extreme that they name: `diag_offsets`: in every draw some group starts at 12000 and another below 64; the others anywhere in the range, blocks may intersect.
All inputs are finite; a program needn't handle non-finite values.
Results may differ from a plain program's by a relative error of at most 0.0003.
Values sent between devices are 32-bit elements; how exact they have to be, the bound alone decides.
A program may use at most 64 MiB of HBM per device.

v0:
```python
import jax
import jax.numpy as jnp
from jax import lax
from jax.sharding import PartitionSpec as P

M = 256
KB = 32
RB = 8192


FILL = 1e30


def passed_along(shard, axis, by):
    size = lax.axis_size(axis)
    pairs = [(i, i + by) for i in range(size) if 0 <= i + by < size]
    return lax.ppermute(shard, axis, pairs)


def window_stats(extended):
    count = extended.shape[0] // M
    blocks = jnp.concatenate([extended, jnp.zeros((M,), jnp.float32)]).reshape(count + 1, M)
    row_ids = lax.broadcasted_iota(jnp.int32, (M, M), 0)
    col_ids = lax.broadcasted_iota(jnp.int32, (M, M), 1)
    upper = (row_ids >= col_ids).astype(jnp.float32)
    lower = (row_ids < col_ids).astype(jnp.float32)

    def window_sums(values):
        head = jnp.dot(
            values[:-1], upper, precision=lax.Precision.HIGHEST, preferred_element_type=jnp.float32
        )
        after = jnp.dot(
            values[1:], lower, precision=lax.Precision.HIGHEST, preferred_element_type=jnp.float32
        )
        return (head + after).reshape(-1)

    first = window_sums(blocks) / M
    second = window_sums(blocks * blocks) / M
    return (first, 1.0 / jnp.sqrt(second - first * first + 1e-05))


def hankel(vector, height, width):
    span = height + width
    tiled = jnp.tile(vector, height + 1)[: height * (span + 1)]
    return tiled.reshape(height, span + 1)[:, :width]


def skew(matrix):
    height, width = matrix.shape
    padded = jnp.concatenate([matrix, jnp.full((height, height), FILL, matrix.dtype)], axis=1)
    flat = padded.reshape(-1)[: height * (width + height - 1)]
    return flat.reshape(height, width + height - 1)


def running_sums(values):
    height, width = values.shape
    inner = 128
    grouped = values.reshape(height, width // inner, inner)
    within = jnp.cumsum(grouped, axis=2) - grouped
    totals = jnp.sum(grouped, axis=2)
    before = jnp.cumsum(totals, axis=1) - totals
    return ((within + before[:, :, None]).reshape(height, width), jnp.sum(totals, axis=1))


def block_terms(extended, offset, row_start, rows):
    leading = lax.dynamic_slice_in_dim(extended, row_start, rows + M)
    partner = hankel(
        lax.dynamic_slice_in_dim(extended, row_start + offset, KB + rows + M), KB, rows + M
    )
    return leading[None, M:] * partner[:, M:] - leading[None, :rows] * partner[:, :rows]


def first_products(extended, offset):
    partner = hankel(lax.dynamic_slice_in_dim(extended, offset, KB + M), KB, M)
    return jnp.dot(
        partner, extended[:M], precision=lax.Precision.HIGHEST, preferred_element_type=jnp.float32
    )


def sweep(extended, means, spreads, offset, exclusion_width, limit, start, segment):
    rows = min(RB, segment)
    diag_ids = lax.broadcasted_iota(jnp.int32, (KB, rows), 0)
    row_ids = lax.broadcasted_iota(jnp.int32, (KB, rows), 1)

    def advance(index, carry):
        current, row_best, column_best = carry
        row_start = (index * rows).astype(jnp.int32)
        change = block_terms(extended, offset, row_start, rows)
        running, total = running_sums(change)
        products = current[:, None] + running
        mean_row = lax.dynamic_slice_in_dim(means, row_start, rows)
        spread_row = lax.dynamic_slice_in_dim(spreads, row_start, rows)
        mean_pair = hankel(lax.dynamic_slice_in_dim(means, row_start + offset, KB + rows), KB, rows)
        spread_pair = hankel(
            lax.dynamic_slice_in_dim(spreads, row_start + offset, KB + rows), KB, rows
        )
        corr = (products / M - mean_row[None, :] * mean_pair) * (spread_row[None, :] * spread_pair)
        distance = jnp.sqrt(1.0 - corr)
        partner_pos = row_start + offset + diag_ids + row_ids
        counted = (offset + diag_ids >= exclusion_width) & (partner_pos < limit)
        masked = jnp.where(counted, distance, FILL)
        row_best = lax.dynamic_update_slice_in_dim(row_best, jnp.min(masked, axis=0), row_start, 0)
        column_block = jnp.min(skew(masked), axis=0)
        column_start = row_start + offset
        previous = lax.dynamic_slice_in_dim(column_best, column_start, rows + KB - 1)
        column_best = lax.dynamic_update_slice_in_dim(
            column_best, jnp.minimum(previous, column_block), column_start, 0
        )
        return (current + total, row_best, column_best)

    initial = (
        start,
        jnp.full((segment,), FILL, jnp.float32),
        jnp.full((extended.shape[0],), FILL, jnp.float32),
    )
    result = lax.fori_loop(0, segment // rows, advance, initial)
    return (result[1], result[2])


def on_device(series, tail, diag_offsets, exclusion):
    segment = series.shape[0]
    reach = segment // 2 + segment // 4
    position = lax.axis_index("tm")
    final_place = lax.axis_size("tm") - 1
    ahead = passed_along(series[:reach], "tm", -1)
    tail_block = jnp.concatenate([tail, jnp.zeros((reach - tail.shape[0],), jnp.float32)])
    ahead = jnp.where(position == final_place, tail_block, ahead)
    extended = jnp.concatenate([series, ahead])
    means, spreads = window_stats(extended)
    offset = diag_offsets[0]
    exclusion_width = exclusion[0]
    limit = jnp.where(position == final_place, segment, segment + reach).astype(jnp.int32)
    start = first_products(extended, offset)
    row_best, column_best = sweep(
        extended, means, spreads, offset, exclusion_width, limit, start, segment
    )
    spilled = passed_along(column_best[segment:], "tm", 1)
    spilled = jnp.where(position == 0, FILL, spilled)
    spilled = jnp.concatenate([spilled, jnp.full((segment - reach,), FILL, jnp.float32)])
    owned = jnp.minimum(jnp.minimum(row_best, column_best[:segment]), spilled)
    groups = lax.axis_size("diag")
    share = segment // groups
    received = lax.all_to_all(owned, "diag", split_axis=0, concat_axis=0, tiled=True)
    return jnp.min(received.reshape(groups, share), axis=0)


def solution(mesh):
    in_specs = (P("tm"), P(), P("diag"), P())
    out_specs = P(("tm", "diag"))
    return jax.shard_map(
        on_device, mesh=mesh, in_specs=in_specs, out_specs=out_specs, check_vma=False
    )
```

profile of v0, /device:TPU:24, one launch (start us, length us, event | category | flops | bytes accessed | tf_op | source)
XLA Modules:
  0.0 118.3 jit_solution(3429441670528963610)
XLA Ops:
  0.0 0.9 slice.126
  0.9 4.3 %collective-permute-start = (f32[12288]{0:T(1024)S(1)}, f32[12288]{0:T(1024)S(1)}, u32[]{:S(2)}, u32[]{:S(2)}) collective-permute-start(f32[12288]{0:T(1024)S(1)} %slice.126), channel_id=1, source_target_pairs={{16,0},{32,16},{48,32},{64,48},{80,64},{96,80},{112,96},{128,112},... | collective-permute-start | bytes 147464 | tf_op jit(solution)/shard_map/ppermute | solution.py:17
  5.8 1.1 collective-permute-done
  6.9 0.7 pad_select_fusion
  7.6 0.8 pad_maximum_fusion
  8.4 0.8 fusion.23
  10.8 0.7 convolution_bitcast_fusion
  11.6 0.6 broadcast_in_dim.41
  12.2 0.7 broadcast_in_dim.42
  12.8 67.8 %while.19 = (s32[]{:T(128)}, f32[32]{0:T(128)}, f32[16384]{0:T(1024)}, f32[28672]{0:T(1024)}, f32[28672]{0:T(1024)S(1)}, /*index=5*/s32[]{:T(128)}, s32[]{:T(128...) while((s32[]{:T(128)}, f32[32]{0:T(128)}, ...), condition=%wide.region_7.8_spmd.clone.clone, body=%wide.region_0.7_spmd.clone.clone.sunk | while | flops 39443432 | bytes 52372300 | solution.py:116
  14.0 0.4 tile.103
  14.5 1.7 %reshape.124 = f32[32,8225]{1,0:T(8,128)} reshape(f32[263200]{0:T(1024)S(1)} %slice.198) | data formatting | bytes 2105600 | tf_op jit(solution)/shard_map/while/body/eval_jaxpr/reshape | solution.py:45
  16.3 0.4 tile.101
  16.8 1.7 %reshape.123 = f32[32,8225]{1,0:T(8,128)} reshape(f32[263200]{0:T(1024)S(1)} %slice.197) | data formatting | bytes 2105600 | tf_op jit(solution)/shard_map/while/body/eval_jaxpr/reshape | solution.py:45
  18.6 0.8 tile.99
  19.5 0.7 reshape.122
  20.2 0.8 fusion.40
  21.3 0.3 reduce_sum.34
  21.6 14.7 %reduce_window_sum.39 = f32[32,64,128]{2,1,0:T(8,128)} reduce-window(f32[32,64,128]{2,1,0:T(8,128)S(1)} %bitcast.59, f32[]{:T(128)} %constant.96.clone.1..sunk), window={size=1x1x128 pad=0_0x0_0x127_0}, to_apply=%region_2.2 | reduce-window | flops 33292288 | bytes 2097156 | tf_op jit(solution)/shard_map/while/body/eval_jaxpr/jit(cumsum)/reduce_window_sum | solution.py:59
  36.9 0.7 copy-done
  37.6 5.0 %fusion.41 = (f32[8192]{0:T(1024)S(1)}, f32[32,8192]{1,0:T(8,128)S(1)}) fusion(f32[32,8225]{1,0:T(8,128)} %reshape.123, f32[8192]{0:T(1024)S(1)} %dynamic_slice.85, f32[32,8225]{1,0:T(8,128)S(1)} %copy-done, f32[8192]{0:T(1024)S(1)} %dynamic_slice.87, f32[4,8,64,128]{3,2,1,0:T(8,128)S(1)} %bitcast.63, f32[32,8192]{1,0:T(8,128)S(1)} %get-tuple-element.361, ...), kind=kLoop, calls=%fused_computation.45.clone.1 | loop fusion | flops 4448256 | bytes 6389904 | tf_op jit(solution)/shard_map/while/body/eval_jaxpr/reduce_min | solution.py:102
  42.6 0.6 copy-done.7
  43.2 0.5 dynamic_update_slice.22
  43.8 0.4 reshape.125
  44.4 0.7 reshape.126
  45.2 1.6 %minimum_dynamic-update-slice_fusion.2 = f32[28672]{0:T(1024)} fusion(f32[28672]{0:T(1024)} %get-tuple-element.386, s32[]{:T(128)S(6)} %select_n.81, f32[8223]{0:T(1024)S(1)} %reduce_min.44), kind=kLoop, calls=%fused_computation.22.clone.1 | loop fusion | flops 8223 | bytes 106624 | tf_op jit(solution)/shard_map/while/body/eval_jaxpr/dynamic_update_slice | solution.py:106
  47.9 0.4 tile.103
  48.5 1.7 %reshape.124 = f32[32,8225]{1,0:T(8,128)} reshape(f32[263200]{0:T(1024)S(1)} %slice.198) | data formatting | bytes 2105600 | tf_op jit(solution)/shard_map/while/body/eval_jaxpr/reshape | solution.py:45
  50.3 0.4 tile.101
  50.8 1.7 %reshape.123 = f32[32,8225]{1,0:T(8,128)} reshape(f32[263200]{0:T(1024)S(1)} %slice.197) | data formatting | bytes 2105600 | tf_op jit(solution)/shard_map/while/body/eval_jaxpr/reshape | solution.py:45
  52.5 0.8 tile.99
  53.5 0.7 reshape.122
  54.2 0.8 fusion.40
  55.2 0.3 reduce_sum.34
  55.5 14.7 %reduce_window_sum.39 = f32[32,64,128]{2,1,0:T(8,128)} reduce-window(f32[32,64,128]{2,1,0:T(8,128)S(1)} %bitcast.59, f32[]{:T(128)} %constant.96.clone.1..sunk), window={size=1x1x128 pad=0_0x0_0x127_0}, to_apply=%region_2.2 | reduce-window | flops 33292288 | bytes 2097156 | tf_op jit(solution)/shard_map/while/body/eval_jaxpr/jit(cumsum)/reduce_window_sum | solution.py:59
  70.8 0.7 copy-done
  71.5 5.0 %fusion.41 = (f32[8192]{0:T(1024)S(1)}, f32[32,8192]{1,0:T(8,128)S(1)}) fusion(f32[32,8225]{1,0:T(8,128)} %reshape.123, f32[8192]{0:T(1024)S(1)} %dynamic_slice.85, f32[32,8225]{1,0:T(8,128)S(1)} %copy-done, f32[8192]{0:T(1024)S(1)} %dynamic_slice.87, f32[4,8,64,128]{3,2,1,0:T(8,128)S(1)} %bitcast.63, f32[32,8192]{1,0:T(8,128)S(1)} %get-tuple-element.361, ...), kind=kLoop, calls=%fused_computation.45.clone.1 | loop fusion | flops 4448256 | bytes 6389904 | tf_op jit(solution)/shard_map/while/body/eval_jaxpr/reduce_min | solution.py:102
  76.6 0.6 copy-done.7
  77.2 0.4 dynamic_update_slice.22
  77.7 0.4 reshape.125
  78.2 0.7 reshape.126
  79.0 1.6 %minimum_dynamic-update-slice_fusion.2 = f32[28672]{0:T(1024)} fusion(f32[28672]{0:T(1024)} %get-tuple-element.386, s32[]{:T(128)S(6)} %select_n.81, f32[8223]{0:T(1024)S(1)} %reduce_min.44), kind=kLoop, calls=%fused_computation.22.clone.1 | loop fusion | flops 8223 | bytes 106624 | tf_op jit(solution)/shard_map/while/body/eval_jaxpr/dynamic_update_slice | solution.py:106
  80.6 0.8 slice.138
  81.4 1.9 %collective-permute-start.1 = (f32[12288]{0:T(1024)S(1)}, f32[12288]{0:T(1024)S(1)}, u32[]{:S(2)}, u32[]{:S(2)}) collective-permute-start(f32[12288]{0:T(1024)S(1)} %slice.138), channel_id=1, source_target_pairs={{0,16},{16,32},{32,48},{48,64},{64,80},{80,96},{96,112},{112,128},... | collective-permute-start | bytes 147464 | tf_op jit(solution)/shard_map/ppermute | solution.py:17
  83.3 5.6 %collective-permute-done.1 = f32[12288]{0:T(1024)S(1)} collective-permute-done((f32[12288]{0:T(1024)S(1)}, f32[12288]{0:T(1024)S(1)}, u32[]{:S(2)}, u32[]{:S(2)}) %collective-permute-start.1) | collective-permute-done | bytes 49184 | tf_op jit(solution)/shard_map/ppermute | solution.py:17
  89.0 0.9 pad_minimum_fusion
  89.8 27.8 %all_to_all.9 = f32[16,1024,1]{1,2,0:T(1,128)S(1)} all-to-all(f32[16,1024,1]{1,2,0:T(1,128)S(1)} %bitcast.68), channel_id=1, replica_groups=mesh['tm'=32,'diag'=16] {'diag'}, dimensions={0} | all-to-all | bytes 131072 | tf_op jit(solution)/shard_map/all_to_all | solution.py:143
  117.7 0.6 reduce_min.35
  (89 shorter events, 5.2 us)
Async XLA Ops:
  0.0 9.5 %copy-start.3 = (f32[16384]{0:T(1024)S(1)}, f32[16384]{0:T(1024)}, u32[]{:S(2)}) copy-start(f32[16384]{0:T(1024)} %param.6) | copy-start | bytes 196612
  0.9 6.0 %collective-permute-start = (f32[12288]{0:T(1024)S(1)}, f32[12288]{0:T(1024)S(1)}, u32[]{:S(2)}, u32[]{:S(2)}) collective-permute-start(f32[12288]{0:T(1024)S(1)} %slice.126), channel_id=1, source_target_pairs={{16,0},{32,16},{48,32},{64,48},{80,64},{96,80},{112,96},{128,112},... | collective-permute-start | bytes 147464 | tf_op jit(solution)/shard_map/ppermute | solution.py:17
  9.6 1.2 slice-start
  12.8 0.7 copy-start.1
  36.3 1.2 %copy-start = (f32[32,8225]{1,0:T(8,128)S(1)}, f32[32,8225]{1,0:T(8,128)}, u32[]{:S(2)}) copy-start(f32[32,8225]{1,0:T(8,128)} %reshape.124) | copy-start | bytes 3158404 | tf_op jit(solution)/shard_map/while
  36.3 1.2 %copy-start.6 = (f32[32]{0:T(128)S(1)}, f32[32]{0:T(128)}, u32[]{:S(2)}) copy-start(f32[32]{0:T(128)} %get-tuple-element.384) | copy-start | bytes 388 | tf_op jit(solution)/shard_map/while
  37.5 5.1 %copy-start.8 = (f32[32]{0:T(128)S(1)}, f32[32]{0:T(128)}, u32[]{:S(2)}) copy-start(f32[32]{0:T(128)} %get-tuple-element.360) | copy-start | bytes 388 | tf_op jit(solution)/shard_map/while
  37.6 5.7 %copy-start.4 = (f32[16384]{0:T(1024)S(1)}, f32[16384]{0:T(1024)}, u32[]{:S(2)}) copy-start(f32[16384]{0:T(1024)} %get-tuple-element.385) | copy-start | bytes 196612 | tf_op jit(solution)/shard_map/while
  42.6 0.6 copy-start.7
  43.7 0.6 copy-start.5
  45.0 1.8 %copy-start.2 = (f32[28672]{0:T(1024)S(1)}, f32[28672]{0:T(1024)}, u32[]{:S(2)}) copy-start(f32[28672]{0:T(1024)} %copy-done.1) | copy-start | bytes 344068 | tf_op jit(solution)/shard_map/while
  46.8 0.7 copy-start.1
  70.3 1.2 %copy-start = (f32[32,8225]{1,0:T(8,128)S(1)}, f32[32,8225]{1,0:T(8,128)}, u32[]{:S(2)}) copy-start(f32[32,8225]{1,0:T(8,128)} %reshape.124) | copy-start | bytes 3158404 | tf_op jit(solution)/shard_map/while
  70.3 1.2 %copy-start.6 = (f32[32]{0:T(128)S(1)}, f32[32]{0:T(128)}, u32[]{:S(2)}) copy-start(f32[32]{0:T(128)} %get-tuple-element.384) | copy-start | bytes 388 | tf_op jit(solution)/shard_map/while
  71.5 5.1 %copy-start.8 = (f32[32]{0:T(128)S(1)}, f32[32]{0:T(128)}, u32[]{:S(2)}) copy-start(f32[32]{0:T(128)} %get-tuple-element.360) | copy-start | bytes 388 | tf_op jit(solution)/shard_map/while
  71.5 5.7 %copy-start.4 = (f32[16384]{0:T(1024)S(1)}, f32[16384]{0:T(1024)}, u32[]{:S(2)}) copy-start(f32[16384]{0:T(1024)} %get-tuple-element.385) | copy-start | bytes 196612 | tf_op jit(solution)/shard_map/while
  76.6 0.6 copy-start.7
  77.6 0.6 copy-start.5
  78.9 1.8 %copy-start.2 = (f32[28672]{0:T(1024)S(1)}, f32[28672]{0:T(1024)}, u32[]{:S(2)}) copy-start(f32[28672]{0:T(1024)} %copy-done.1) | copy-start | bytes 344068 | tf_op jit(solution)/shard_map/while
  81.4 7.5 %collective-permute-start.1 = (f32[12288]{0:T(1024)S(1)}, f32[12288]{0:T(1024)S(1)}, u32[]{:S(2)}, u32[]{:S(2)}) collective-permute-start(f32[12288]{0:T(1024)S(1)} %slice.138), channel_id=1, source_target_pairs={{0,16},{16,32},{32,48},{48,64},{64,80},{80,96},{96,112},{112,128},... | collective-permute-start | bytes 147464 | tf_op jit(solution)/shard_map/ppermute | solution.py:17
where the time goes:
time: 119 us; the launch traced here: 118 us
  other arithmetic  49.7 us (42%)
  blocking collectives  27.8 us (23%)
  local copies, waits for them, and re-layouts  23.7 us (20%)
  waiting for transfers between devices  6.68 us (6%)
  starting transfers between devices  6.18 us (5%)
  loops' own time  1.69 us (1%)
  matrix products  1.64 us (1%)
    another operation x2, other arithmetic, running_sums(): within = jnp.cumsum(grouped, axis=2) - grouped  29.4 us
    all_to_all x1, blocking collectives, on_device(): lax.all_to_all(owned, 'diag', split_axis=0, concat_axis=0, tiled=True)  27.8 us
    reduce_min x2, other arithmetic, advance(): jnp.min(masked, axis=0)  10.1 us
    reshape x7, local copies, waits for them, and re-layouts, hankel(): return tiled.reshape(height, span + 1)[:, :width]  8.32 us
    ppermute x2, waiting for transfers between devices, passed_along(): return lax.ppermute(shard, axis, pairs)  6.68 us
    ppermute x2, starting transfers between devices, passed_along(): return lax.ppermute(shard, axis, pairs)  6.18 us
    another operation x14, local copies, waits for them, and re-layouts, hankel(): tiled = jnp.tile(vector, height + 1)[:height * (span + 1)]  4.04 us
    dynamic_update_slice x2, other arithmetic, advance(): lax.dynamic_update_slice_in_dim(column_best, jnp.minimum(previous, column...  3.26 us
  transfers between devices with their start and end apart: 2, of which 2 were waited for; matrix products, arithmetic and copies ran while one was open for 0% of the time, Pallas kernels for 0%

commit v1 on v0

v1 whole, which is shorter than its diff:
```python
import functools

import jax
import jax.numpy as jnp
from jax import lax
from jax.experimental import pallas as pl
from jax.experimental.pallas import tpu as pltpu
from jax.sharding import PartitionSpec as P

F32 = jnp.float32
BF16 = jnp.bfloat16
MESH = pl.DeviceIdType.MESH

M = 256
KB = 32
LANES = 128
FILL = 1e30

HALO = 96
SEG = 128
OWN = 8
REGION = 2 * HALO + OWN + 16
EXT = 2 * HALO + SEG + 16
PRODUCT_BLOCKS = OWN + 2


def hop(k):
    return (k + 1) // 2 * (1 if k % 2 else -1)


def split2(v):
    high = v.astype(BF16)
    return high, (v - high.astype(F32)).astype(BF16)


def window_weights():
    r = lax.broadcasted_iota(jnp.int32, (256, 256), 0) & 127
    c = lax.broadcasted_iota(jnp.int32, (256, 256), 1)
    from_c = jnp.where(r >= c, 1.0, 0.0)
    before_c = jnp.where(r < c - 128, 1.0, 0.0)
    return jnp.where(c < 128, from_c, before_c).astype(BF16)


def window_stats(x_ref, w_ref, mean_ref, a_ref, b_ref):
    def window_sums(v):
        high, mid = split2(v)
        low = (v - high.astype(F32) - mid.astype(F32)).astype(BF16)
        g = jnp.dot(jnp.concatenate([high, mid], axis=1), w_ref[...], preferred_element_type=F32)
        g = g + jnp.dot(low, w_ref[:128, :], preferred_element_type=F32)
        from_c, before_c = g[:, :128], g[:, 128:]
        n = v.shape[0]
        return from_c[: n - 2] + (from_c + before_c)[1 : n - 1] + before_c[2:]

    x = x_ref[...]
    n = x.shape[0] - 2
    first = window_sums(x) * (1.0 / M)
    second = window_sums(x * x) * (1.0 / M)
    spread = 1.0 / jnp.sqrt(second - first * first + 1e-5)
    mean_ref[:n, :] = first
    a_ref[:n, :] = spread * (1.0 / M)
    b_ref[:n, :] = first * spread


def align(ref, z_ref, row, lane):
    n = z_ref.shape[0]
    shift = (128 - lane) & 127
    here = pltpu.roll(ref[pl.ds(row, n), :], shift, 1)
    after = pltpu.roll(ref[pl.ds(row + 1, n), :], shift, 1)
    lanes = lax.broadcasted_iota(jnp.int32, (n, 128), 1)
    z_ref[...] = jnp.where(lanes < 128 - lane, here, after)


def hankel(z_ref, blocks, emit):
    lanes = lax.broadcasted_iota(jnp.int32, (KB, 128), 1)
    subs = lax.broadcasted_iota(jnp.int32, (KB, 128), 0)
    keep = lanes < 97 + subs
    last = None
    for j in range(blocks + 1):
        rolled = pltpu.roll(
            jnp.broadcast_to(z_ref[j : j + 1, :], (KB, 128)), 97, 1, stride=1, stride_axis=0
        )
        if last is not None:
            emit(j - 1, jnp.where(keep, last, rolled))
        last = rolled


def band(beta, exclusion, pos0, total, x_ref, a_ref, b_ref, mean_ref, w_ref, zx, za, zb, lhs, sums, best):
    start = HALO * 128 + beta
    row = lax.shift_right_arithmetic(start, 7)
    lane = start & 127
    align(x_ref, zx, row, lane)
    align(a_ref, za, row, lane)
    align(b_ref, zb, row, lane)

    def own_row(ref, j):
        return jnp.broadcast_to(ref[HALO + j : HALO + j + 1, :], (KB, 128))

    def emit_products(j, y):
        high, low = split2(y * own_row(x_ref, j))
        lhs[KB * j : KB * j + KB, :128] = high
        lhs[KB * j : KB * j + KB, 128:] = low

    hankel(zx, PRODUCT_BLOCKS, emit_products)
    sums[...] = jnp.dot(lhs[...], w_ref[...], preferred_element_type=F32)

    delta = beta + 31 - lax.broadcasted_iota(jnp.int32, (KB, 128), 0)
    far = jnp.abs(delta) >= exclusion
    partner = pos0 + delta + lax.broadcasted_iota(jnp.int32, (KB, 128), 1)
    scaled = {}
    hankel(za, OWN, scaled.__setitem__)

    def emit_scores(j, y):
        here = slice(KB * j, KB * j + KB)
        middle = slice(KB * (j + 1), KB * (j + 2))
        ahead = slice(KB * (j + 2), KB * (j + 3))
        products = sums[here, :128] + (sums[middle, :128] + sums[middle, 128:]) + sums[ahead, 128:]
        score = products * scaled[j] - own_row(mean_ref, j) * y
        there = partner + 128 * j
        counted = far & (there >= 0) & (there < total)
        best[here, :] = jnp.maximum(best[here, :], jnp.where(counted, score, -FILL))

    hankel(zb, OWN, emit_scores)


def finish(best, a_ref, out_ref):
    rows = [jnp.max(best[KB * j : KB * j + KB, :], axis=0, keepdims=True) for j in range(OWN)]
    top = jnp.concatenate(rows, axis=0)
    corr = top * (a_ref[HALO : HALO + OWN, :] * float(M))
    out_ref[...] = jnp.where(top < -0.1 * FILL, FILL, jnp.sqrt(1.0 - corr))


def kernel(
    series, tail, offset, exclusion, out,
    ext, x_ref, mean_ref, a_ref, b_ref, w_ref, zx, za, zb, lhs, sums, best,
    mine, gathered, halo_send, halo_recv, off_send, off_recv,
    *, n_tm, n_diag, total,
):
    tm = lax.axis_index("tm")
    z = lax.axis_index("diag")
    has_prev = tm > 0
    has_next = tm < n_tm - 1

    def peer(h):
        return (tm, lax.rem(z + h + n_diag, n_diag))

    barrier = pltpu.get_barrier_semaphore()

    @pl.when(has_prev)
    def _():
        pl.semaphore_signal(barrier, inc=1, device_id=(tm - 1, z), device_id_type=MESH)

    @pl.when(has_next)
    def _():
        pl.semaphore_signal(barrier, inc=1, device_id=(tm + 1, z), device_id_type=MESH)

    for k in range(n_diag - 1, 0, -1):
        pl.semaphore_signal(barrier, inc=1, device_id=peer(hop(k)), device_id_type=MESH)

    mine[0, 0] = offset[0]
    gathered[0, 0] = offset[0]
    ext[HALO : HALO + SEG, :] = series[...]
    ext[2 * HALO + SEG :, :] = jnp.zeros((EXT - 2 * HALO - SEG, 128), F32)
    w_ref[...] = window_weights()
    best[...] = jnp.full(best.shape, -FILL, F32)

    @pl.when(jnp.logical_not(has_prev))
    def _():
        ext[:HALO, :] = jnp.zeros((HALO, 128), F32)

    @pl.when(jnp.logical_not(has_next))
    def _():
        ext[HALO + SEG : HALO + SEG + 2, :] = tail[...]
        ext[HALO + SEG + 2 : 2 * HALO + SEG, :] = jnp.zeros((HALO - 2, 128), F32)

    edge = has_prev.astype(jnp.int32) + has_next.astype(jnp.int32)
    pl.semaphore_wait(barrier, n_diag - 1 + edge)

    def offset_copy(k):
        return pltpu.make_async_remote_copy(
            mine, gathered.at[pl.ds(k, 1)], off_send.at[k], off_recv.at[k],
            device_id=peer(-hop(k)), device_id_type=MESH,
        )

    to_prev = pltpu.make_async_remote_copy(
        series.at[pl.ds(0, HALO)], ext.at[pl.ds(HALO + SEG, HALO)], halo_send.at[0], halo_recv.at[0],
        device_id=(tm - 1, z), device_id_type=MESH,
    )
    to_next = pltpu.make_async_remote_copy(
        series.at[pl.ds(SEG - HALO, HALO)], ext.at[pl.ds(0, HALO)], halo_send.at[1], halo_recv.at[1],
        device_id=(tm + 1, z), device_id_type=MESH,
    )

    for k in range(n_diag - 1, 0, -1):
        offset_copy(k).start()

    @pl.when(has_prev)
    def _():
        to_prev.start()

    @pl.when(has_next)
    def _():
        to_next.start()

    @pl.when(has_next)
    def _():
        to_prev.wait_recv()

    @pl.when(has_prev)
    def _():
        to_next.wait_recv()

    x_ref[...] = ext[pl.ds(pl.multiple_of(OWN * z, OWN), REGION), :]
    window_stats(x_ref, w_ref, mean_ref, a_ref, b_ref)
    pos0 = (tm * SEG + z * OWN) * 128

    def group(k, carry):
        @pl.when(k > 0)
        def _():
            pltpu.make_async_remote_copy(
                mine, gathered.at[pl.ds(k, 1)], off_send.at[k], off_recv.at[k],
                device_id=peer(1), device_id_type=MESH,
            ).wait_recv()

        first = gathered[k, 0]

        def side(d, c):
            beta = first + d * (-2 * first - (KB - 1))
            band(
                beta, exclusion[0], pos0, total,
                x_ref, a_ref, b_ref, mean_ref, w_ref, zx, za, zb, lhs, sums, best,
            )
            return c

        return lax.fori_loop(0, 2, side, carry)

    lax.fori_loop(0, n_diag, group, 0)
    finish(best, a_ref, out)

    for k in range(1, n_diag):
        offset_copy(k).wait_send()

    @pl.when(has_prev)
    def _():
        to_prev.wait_send()

    @pl.when(has_next)
    def _():
        to_next.wait_send()


def solution(mesh):
    n_tm, n_diag = mesh.shape["tm"], mesh.shape["diag"]

    def on_device(series, tail, diag_offsets, exclusion):
        total = series.shape[0] * n_tm
        vmem = pl.BlockSpec(memory_space=pltpu.VMEM)
        smem = pl.BlockSpec(memory_space=pltpu.SMEM)
        rows = pl.pallas_call(
            functools.partial(kernel, n_tm=n_tm, n_diag=n_diag, total=total),
            out_shape=jax.ShapeDtypeStruct((OWN, 128), F32),
            in_specs=[vmem, vmem, smem, smem],
            out_specs=vmem,
            scratch_shapes=[
                pltpu.VMEM((EXT, 128), F32),
                pltpu.VMEM((REGION, 128), F32),
                pltpu.VMEM((REGION, 128), F32),
                pltpu.VMEM((REGION, 128), F32),
                pltpu.VMEM((REGION, 128), F32),
                pltpu.VMEM((256, 256), BF16),
                pltpu.VMEM((16, 128), F32),
                pltpu.VMEM((16, 128), F32),
                pltpu.VMEM((16, 128), F32),
                pltpu.VMEM((KB * PRODUCT_BLOCKS, 256), BF16),
                pltpu.VMEM((KB * PRODUCT_BLOCKS, 256), F32),
                pltpu.VMEM((KB * OWN, 128), F32),
                pltpu.SMEM((1, 128), jnp.int32),
                pltpu.SMEM((16, 128), jnp.int32),
                pltpu.SemaphoreType.DMA((2,)),
                pltpu.SemaphoreType.DMA((2,)),
                pltpu.SemaphoreType.DMA((16,)),
                pltpu.SemaphoreType.DMA((16,)),
            ],
            compiler_params=pltpu.CompilerParams(collective_id=0, has_side_effects=True),
            name="profile_rows",
        )(
            series.reshape(SEG, 128),
            tail.reshape(M // 128, 128),
            diag_offsets,
            exclusion,
        )
        return rows.reshape(-1)

    in_specs = (P("tm"), P(), P("diag"), P())
    out_specs = P(("tm", "diag"))
    return jax.shard_map(
        on_device, mesh=mesh, in_specs=in_specs, out_specs=out_specs, check_vma=False
    )
```

time: 119 us -> 37.2 us (0.31)
  the two profiles are of different devices: /device:TPU:24 before, /device:TPU:1 now
where the time goes in v1:
time: 37.2 us; the launch traced here: 37 us
  Pallas kernels  34.4 us (92%)
  between operations  1.3 us (3%)
  local copies, waits for them, and re-layouts  1.28 us (3%)
    pallas_call x1, Pallas kernels, on_device(): pl.pallas_call(functools.partial(kernel, n_tm=n_tm, n_diag=n_diag, total=...  34.4 us
    unnamed x1, local copies, waits for them, and re-layouts  1.28 us

profile of v1, /device:TPU:1, one launch (start us, length us, event | category | flops | bytes accessed | tf_op | source)
XLA Modules:
  0.0 37.0 jit_solution(11890200096393424439)
XLA Ops:
  1.3 34.4 %profile_rows.1 = f32[8,128]{1,0:T(8,128)} custom-call(f32[128,128]{1,0:T(8,128)} %bitcast.3, f32[2,128]{1,0:T(2,128)} %bitcast.5, s32[1]{0:T(128)S(6)} %copy.6.offset, s32[1]{0:T(128)S(6)} %copy.7.exclusion), custom_call_target="tpu_custom_call" | custom-call | tf_op jit(solution)/shard_map/profile_rows/pallas_call | solution.py:258
  35.7 1.3 %copy.8 = f32[1024]{0:T(1024)} copy(f32[1024]{0:T(1024)} %bitcast.4) | data formatting | bytes 8192

commit v2 on v1

v2 whole, which is shorter than its diff:
```python
import functools

import jax
import jax.numpy as jnp
from jax import lax
from jax.experimental import pallas as pl
from jax.experimental.pallas import tpu as pltpu
from jax.sharding import PartitionSpec as P

F32 = jnp.float32
BF16 = jnp.bfloat16
MESH = pl.DeviceIdType.MESH

M = 256
KB = 32
LANES = 128
FILL = 1e30

HALO = 96
SEG = 128
OWN = 8
REGION = 2 * HALO + OWN + 16
SKEWED = REGION - 8
EXT = 2 * HALO + SEG + 16
STEPS = KB // 8
SCORE_BLOCKS = OWN + 1
NEAR = 4


def hop(k):
    return (k + 1) // 2 * (1 if k % 2 else -1)


def split2(v):
    high = v.astype(BF16)
    return high, (v - high.astype(F32)).astype(BF16)


def window_weights():
    r = lax.broadcasted_iota(jnp.int32, (256, 256), 0) & 127
    c = lax.broadcasted_iota(jnp.int32, (256, 256), 1)
    from_c = jnp.where(r >= c, 1.0, 0.0)
    before_c = jnp.where(r < c - 128, 1.0, 0.0)
    return jnp.where(c < 128, from_c, before_c).astype(BF16)


def window_stats(x_ref, w_ref, mean_ref, a_ref, b_ref):
    def window_sums(v):
        high, mid = split2(v)
        low = (v - high.astype(F32) - mid.astype(F32)).astype(BF16)
        g = jnp.dot(jnp.concatenate([high, mid], axis=1), w_ref[...], preferred_element_type=F32)
        g = g + jnp.dot(low, w_ref[:128, :], preferred_element_type=F32)
        from_c, before_c = g[:, :128], g[:, 128:]
        n = v.shape[0]
        return from_c[: n - 2] + (from_c + before_c)[1 : n - 1] + before_c[2:]

    x = x_ref[...]
    n = x.shape[0] - 2
    first = window_sums(x) * (1.0 / M)
    second = window_sums(x * x) * (1.0 / M)
    spread = 1.0 / jnp.sqrt(second - first * first + 1e-5)
    mean_ref[:n, :] = first
    a_ref[:n, :] = spread * (1.0 / M)
    b_ref[:n, :] = first * spread


def own_rows(ref, out_ref):
    n = 16
    here = ref[HALO : HALO + n, :]
    before = ref[HALO - 1 : HALO - 1 + n, :]
    lanes = lax.broadcasted_iota(jnp.int32, (n, 128), 1)
    out_ref[:n, :] = here
    for v in range(1, STEPS):
        shift = 8 * v
        out_ref[n * v : n * v + n, :] = jnp.where(
            lanes < shift, pltpu.roll(before, shift, 1), pltpu.roll(here, shift, 1)
        )


def skewed(pairs):
    lanes = lax.broadcasted_iota(jnp.int32, (8, 128), 1)
    subs = lax.broadcasted_iota(jnp.int32, (8, 128), 0)
    here = lanes < 121 + subs
    batch = SKEWED // 4

    def rows(i, carry):
        start = batch * i
        for ref, out_ref in pairs:
            last = None
            for j in range(batch + 1):
                row = jnp.broadcast_to(ref[pl.ds(start + j, 1), :], (8, 128))
                rolled = pltpu.roll(row, 121, 1, stride=1, stride_axis=0)
                if j:
                    out_ref[pl.ds(pl.multiple_of(8 * (start + j - 1), 8), 8), :] = jnp.where(here, last, rolled)
                last = rolled
        return carry

    lax.fori_loop(0, SKEWED // batch, rows, 0)


def hankel(ref, row, lane, blocks, emit):
    lanes = lax.broadcasted_iota(jnp.int32, (8, 128), 1)
    here = lanes < 128 - lane
    shift = (128 - lane) & 127
    rolled = [
        pltpu.roll(ref[pl.ds(8 * row + 8 * j, 8), :], shift, 1) for j in range(blocks + 1)
    ]
    for j in range(blocks):
        emit(j, jnp.where(here, rolled[j], rolled[j + 1]))


def group_scores(
    first, exclusion, pos0, total, x_ref, a_ref, b_ref, own_x, own_mean, w_ref, scratch, best
):
    subs = lax.broadcasted_iota(jnp.int32, (8, 128), 0)
    lanes = lax.broadcasted_iota(jnp.int32, (8, 128), 1)

    def rows_of(ref, v, j):
        return jnp.broadcast_to(ref[16 * v + j : 16 * v + j + 1, :], (8, 128))

    def at(j, v):
        return slice((STEPS * j + v) * 8, (STEPS * j + v) * 8 + 8)

    sides = []
    for side, (lhs, sums) in enumerate(scratch):
        beta = first if side == 0 else -first - (KB - 1)
        start = HALO * 128 + beta
        row = lax.shift_right_arithmetic(start, 7)
        lane = start & 127
        sides.append((side, beta, row, lane, lhs, sums))

    for _, _, row, lane, lhs, _ in sides:

        def emit_products(j, y, lhs=lhs):
            for v in range(STEPS):
                p = y * rows_of(own_x, v, j)
                lhs[at(j, v), :128] = p
                lhs[at(j, v), 128:] = p - p.astype(BF16).astype(F32)

        hankel(x_ref, row, lane, SCORE_BLOCKS + 2, emit_products)

    for _, _, _, _, lhs, sums in sides:
        sums[...] = jnp.dot(lhs[...], w_ref[...], preferred_element_type=F32)

    for side, beta, row, lane, _, sums in sides:
        partner = pos0 + beta + 7 - subs + lanes
        distance = beta + 7 - subs
        far = [
            (distance + 8 * v >= exclusion) if side == 0 else (-8 * v - distance >= exclusion)
            for v in range(STEPS)
        ]
        scaled = {}
        hankel(a_ref, row, lane, SCORE_BLOCKS, scaled.__setitem__)

        def emit_scores(j, y, side=side, sums=sums, partner=partner, scaled=scaled, far=far):
            inside = partner < total - 128 * j if side == 0 else partner >= -128 * j
            for v in range(STEPS):
                middle = at(j + 1, v)
                products = (
                    sums[at(j, v), :128] + (sums[middle, :128] + sums[middle, 128:]) + sums[at(j + 2, v), 128:]
                )
                score = products * scaled[j] - rows_of(own_mean, v, j) * y
                here = at(j, v)
                best[here, :] = jnp.maximum(best[here, :], jnp.where(inside & far[v], score, -FILL))

        hankel(b_ref, row, lane, SCORE_BLOCKS, emit_scores)


def finish(best, a_ref, out_ref):
    def part(j, v):
        return best[(STEPS * j + v) * 8 : (STEPS * j + v) * 8 + 8, :]

    lanes = lax.broadcasted_iota(jnp.int32, (8, 128), 1)
    tops = [part(j, 0) for j in range(OWN)]
    for v in range(1, STEPS):
        moved = [pltpu.roll(part(j, v), 128 - 8 * v, 1) for j in range(SCORE_BLOCKS)]
        for j in range(OWN):
            tops[j] = jnp.maximum(tops[j], jnp.where(lanes < 128 - 8 * v, moved[j], moved[j + 1]))
    top = jnp.concatenate([jnp.max(t, axis=0, keepdims=True) for t in tops], axis=0)
    corr = top * (a_ref[HALO : HALO + OWN, :] * float(M))
    out_ref[...] = jnp.where(top < -0.1 * FILL, FILL, jnp.sqrt(1.0 - corr))


def kernel(
    series, tail, offset, exclusion, out,
    ext, x_ref, mean_ref, a_ref, b_ref, w_ref, ones_ref,
    x_skew, a_skew, b_skew, own_x, own_mean, lhs0, sums0, lhs1, sums1, best,
    mine, gathered, halo_send, halo_recv, off_send, off_recv,
    *, n_tm, n_diag, total,
):
    tm = lax.axis_index("tm")
    z = lax.axis_index("diag")
    has_prev = tm > 0
    has_next = tm < n_tm - 1

    def peer(h):
        return (tm, lax.rem(z + h + n_diag, n_diag))

    barrier = pltpu.get_barrier_semaphore()

    @pl.when(has_prev)
    def _():
        pl.semaphore_signal(barrier, inc=1, device_id=(tm - 1, z), device_id_type=MESH)

    @pl.when(has_next)
    def _():
        pl.semaphore_signal(barrier, inc=1, device_id=(tm + 1, z), device_id_type=MESH)

    for k in range(2 * NEAR, 0, -1):
        pl.semaphore_signal(barrier, inc=1, device_id=peer(hop(k)), device_id_type=MESH)

    mine[0, 0] = offset[0]
    gathered[0, 0] = offset[0]
    ext[HALO : HALO + SEG, :] = series[...]
    ext[2 * HALO + SEG :, :] = jnp.zeros((EXT - 2 * HALO - SEG, 128), F32)
    w_ref[...] = window_weights()
    ones_ref[...] = w_ref[...].astype(F32)
    scratch = ((lhs0, sums0), (lhs1, sums1))
    best[...] = jnp.full(best.shape, -FILL, F32)

    @pl.when(jnp.logical_not(has_prev))
    def _():
        ext[:HALO, :] = jnp.zeros((HALO, 128), F32)

    @pl.when(jnp.logical_not(has_next))
    def _():
        ext[HALO + SEG : HALO + SEG + 2, :] = tail[...]
        ext[HALO + SEG + 2 : 2 * HALO + SEG, :] = jnp.zeros((HALO - 2, 128), F32)

    edge = has_prev.astype(jnp.int32) + has_next.astype(jnp.int32)
    pl.semaphore_wait(barrier, 2 * NEAR + edge)

    def offset_copy(k):
        h = hop(k)
        near = abs(h) <= NEAR
        source = mine if near else gathered.at[pl.ds(k - 2 * NEAR, 1)]
        to = -h if near else (-NEAR if h > 0 else NEAR)
        return pltpu.make_async_remote_copy(
            source, gathered.at[pl.ds(k, 1)], off_send.at[k], off_recv.at[k],
            device_id=peer(to), device_id_type=MESH,
        )

    to_prev = pltpu.make_async_remote_copy(
        series.at[pl.ds(0, HALO)], ext.at[pl.ds(HALO + SEG, HALO)], halo_send.at[0], halo_recv.at[0],
        device_id=(tm - 1, z), device_id_type=MESH,
    )
    to_next = pltpu.make_async_remote_copy(
        series.at[pl.ds(SEG - HALO, HALO)], ext.at[pl.ds(0, HALO)], halo_send.at[1], halo_recv.at[1],
        device_id=(tm + 1, z), device_id_type=MESH,
    )

    for k in range(2 * NEAR, 0, -1):
        offset_copy(k).start()

    @pl.when(has_prev)
    def _():
        to_prev.start()

    @pl.when(has_next)
    def _():
        to_next.start()

    for k in range(1, 2 * NEAR + 1):
        offset_copy(k).wait_recv()
        if k + 2 * NEAR < n_diag:
            offset_copy(k + 2 * NEAR).start()

    @pl.when(has_next)
    def _():
        to_prev.wait_recv()

    @pl.when(has_prev)
    def _():
        to_next.wait_recv()

    x_ref[...] = ext[pl.ds(pl.multiple_of(OWN * z, OWN), REGION), :]
    window_stats(x_ref, w_ref, mean_ref, a_ref, b_ref)
    skewed(((x_ref, x_skew), (a_ref, a_skew), (b_ref, b_skew)))
    own_rows(x_ref, own_x)
    own_rows(mean_ref, own_mean)
    pos0 = (tm * SEG + z * OWN) * 128

    def group(k, carry):
        @pl.when(k > 2 * NEAR)
        def _():
            pltpu.make_async_remote_copy(
                mine, gathered.at[pl.ds(k, 1)], off_send.at[k], off_recv.at[k],
                device_id=peer(1), device_id_type=MESH,
            ).wait_recv()

        first = gathered[k, 0]

        group_scores(
            first, exclusion[0], pos0, total,
            x_skew, a_skew, b_skew, own_x, own_mean, ones_ref, scratch, best,
        )
        return carry

    lax.fori_loop(0, n_diag, group, 0)
    finish(best, a_ref, out)

    for k in range(1, n_diag):
        offset_copy(k).wait_send()

    @pl.when(has_prev)
    def _():
        to_prev.wait_send()

    @pl.when(has_next)
    def _():
        to_next.wait_send()


def solution(mesh):
    n_tm, n_diag = mesh.shape["tm"], mesh.shape["diag"]

    def on_device(series, tail, diag_offsets, exclusion):
        total = series.shape[0] * n_tm
        vmem = pl.BlockSpec(memory_space=pltpu.VMEM)
        smem = pl.BlockSpec(memory_space=pltpu.SMEM)
        product_rows = KB * (SCORE_BLOCKS + 2)
        side_scratch = [pltpu.VMEM((product_rows, 256), F32)] * 2
        rows = pl.pallas_call(
            functools.partial(kernel, n_tm=n_tm, n_diag=n_diag, total=total),
            out_shape=jax.ShapeDtypeStruct((OWN, 128), F32),
            in_specs=[vmem, vmem, smem, smem],
            out_specs=vmem,
            scratch_shapes=[
                pltpu.VMEM((EXT, 128), F32),
                pltpu.VMEM((REGION, 128), F32),
                pltpu.VMEM((REGION, 128), F32),
                pltpu.VMEM((REGION, 128), F32),
                pltpu.VMEM((REGION, 128), F32),
                pltpu.VMEM((256, 256), BF16),
                pltpu.VMEM((256, 256), F32),
                pltpu.VMEM((8 * SKEWED, 128), F32),
                pltpu.VMEM((8 * SKEWED, 128), F32),
                pltpu.VMEM((8 * SKEWED, 128), F32),
                pltpu.VMEM((16 * STEPS, 128), F32),
                pltpu.VMEM((16 * STEPS, 128), F32),
                *side_scratch,
                *side_scratch,
                pltpu.VMEM((KB * SCORE_BLOCKS, 128), F32),
                pltpu.SMEM((1, 128), jnp.int32),
                pltpu.SMEM((16, 128), jnp.int32),
                pltpu.SemaphoreType.DMA((2,)),
                pltpu.SemaphoreType.DMA((2,)),
                pltpu.SemaphoreType.DMA((16,)),
                pltpu.SemaphoreType.DMA((16,)),
            ],
            compiler_params=pltpu.CompilerParams(collective_id=0, has_side_effects=True),
            name="profile_rows",
        )(
            series.reshape(SEG, 128),
            tail.reshape(M // 128, 128),
            diag_offsets,
            exclusion,
        )
        return rows.reshape(-1)

    in_specs = (P("tm"), P(), P("diag"), P())
    out_specs = P(("tm", "diag"))
    return jax.shard_map(
        on_device, mesh=mesh, in_specs=in_specs, out_specs=out_specs, check_vma=False
    )
```

time: 37.2 us -> 28.3 us (0.76)
  the two profiles are of different devices: /device:TPU:1 before, /device:TPU:18 now
where the time goes in v2:
time: 28.3 us; the launch traced here: 28.1 us
  Pallas kernels  25.5 us (90%)
  between operations  1.3 us (5%)
  local copies, waits for them, and re-layouts  1.28 us (5%)
    pallas_call x1, Pallas kernels, on_device(): pl.pallas_call(functools.partial(kernel, n_tm=n_tm, n_diag=n_diag, total=...  25.5 us
    unnamed x1, local copies, waits for them, and re-layouts  1.28 us

profile of v2, /device:TPU:18, one launch (start us, length us, event | category | flops | bytes accessed | tf_op | source)
XLA Modules:
  0.0 28.1 jit_solution(16901144546894567069)
XLA Ops:
  1.3 25.5 %profile_rows.1 = f32[8,128]{1,0:T(8,128)} custom-call(f32[128,128]{1,0:T(8,128)} %bitcast.3, f32[2,128]{1,0:T(2,128)} %bitcast.5, s32[1]{0:T(128)S(6)} %copy.6.offset, s32[1]{0:T(128)S(6)} %copy.7.exclusion), custom_call_target="tpu_custom_call" | custom-call | tf_op jit(solution)/shard_map/profile_rows/pallas_call | solution.py:323
  26.8 1.3 %copy.8 = f32[1024]{0:T(1024)} copy(f32[1024]{0:T(1024)} %bitcast.4) | data formatting | bytes 8192

commit v3 on v2

--- a/solution.py
+++ b/solution.py
@@ -15,6 +15,7 @@
 KB = 32
 LANES = 128
 FILL = 1e30
+NOWHERE = 1 << 30
 
 HALO = 96
 SEG = 128
@@ -110,7 +111,7 @@
 
 
 def group_scores(
-    first, exclusion, pos0, total, x_ref, a_ref, b_ref, own_x, own_mean, w_ref, scratch, best
+    firsts, exclusion, pos0, total, x_ref, a_ref, b_ref, own_x, own_mean, w_ref, scratch, best
 ):
     subs = lax.broadcasted_iota(jnp.int32, (8, 128), 0)
     lanes = lax.broadcasted_iota(jnp.int32, (8, 128), 1)
@@ -122,48 +123,55 @@
         return slice((STEPS * j + v) * 8, (STEPS * j + v) * 8 + 8)
 
     sides = []
-    for side, (lhs, sums) in enumerate(scratch):
-        beta = first if side == 0 else -first - (KB - 1)
-        start = HALO * 128 + beta
-        row = lax.shift_right_arithmetic(start, 7)
-        lane = start & 127
-        sides.append((side, beta, row, lane, lhs, sums))
-
-    for _, _, row, lane, lhs, _ in sides:
+    for first in firsts:
+        for ahead in (True, False):
+            beta = first if ahead else -first - (KB - 1)
+            start = HALO * 128 + beta
+            sides.append((ahead, beta, lax.shift_right_arithmetic(start, 7), start & 127))
+
+    for (_, _, row, lane), (lhs, _) in zip(sides, scratch):
 
         def emit_products(j, y, lhs=lhs):
-            for v in range(STEPS):
-                p = y * rows_of(own_x, v, j)
-                lhs[at(j, v), :128] = p
-                lhs[at(j, v), 128:] = p - p.astype(BF16).astype(F32)
+            own = jnp.concatenate([rows_of(own_x, v, j) for v in range(STEPS)], axis=0)
+            p = jnp.concatenate([y] * STEPS, axis=0) * own
+            lhs[KB * j : KB * j + KB, :128] = p
+            lhs[KB * j : KB * j + KB, 128:] = p - p.astype(BF16).astype(F32)
 
         hankel(x_ref, row, lane, SCORE_BLOCKS + 2, emit_products)
 
-    for _, _, _, _, lhs, sums in sides:
+    for lhs, sums in scratch[: len(sides)]:
         sums[...] = jnp.dot(lhs[...], w_ref[...], preferred_element_type=F32)
 
-    for side, beta, row, lane, _, sums in sides:
-        partner = pos0 + beta + 7 - subs + lanes
+    masks, scaled, shifted = [], [], []
+    for ahead, beta, row, lane in sides:
         distance = beta + 7 - subs
-        far = [
-            (distance + 8 * v >= exclusion) if side == 0 else (-8 * v - distance >= exclusion)
-            for v in range(STEPS)
-        ]
-        scaled = {}
-        hankel(a_ref, row, lane, SCORE_BLOCKS, scaled.__setitem__)
-
-        def emit_scores(j, y, side=side, sums=sums, partner=partner, scaled=scaled, far=far):
-            inside = partner < total - 128 * j if side == 0 else partner >= -128 * j
-            for v in range(STEPS):
-                middle = at(j + 1, v)
-                products = (
-                    sums[at(j, v), :128] + (sums[middle, :128] + sums[middle, 128:]) + sums[at(j + 2, v), 128:]
-                )
-                score = products * scaled[j] - rows_of(own_mean, v, j) * y
-                here = at(j, v)
-                best[here, :] = jnp.maximum(best[here, :], jnp.where(inside & far[v], score, -FILL))
-
-        hankel(b_ref, row, lane, SCORE_BLOCKS, emit_scores)
+        masks.append((
+            pos0 + distance + lanes,
+            [
+                jnp.where(distance + 8 * v >= exclusion, pos0 + distance + lanes, NOWHERE)
+                if ahead
+                else jnp.where(-8 * v - distance >= exclusion, pos0 + distance + lanes, -NOWHERE)
+                for v in range(STEPS)
+            ],
+        ))
+        scaled.append({})
+        hankel(a_ref, row, lane, SCORE_BLOCKS, scaled[-1].__setitem__)
+        shifted.append({})
+        hankel(b_ref, row, lane, SCORE_BLOCKS, shifted[-1].__setitem__)
+
+    for j in range(SCORE_BLOCKS):
+        for v in range(STEPS):
+            here, middle, after = at(j, v), at(j + 1, v), at(j + 2, v)
+            mean = rows_of(own_mean, v, j)
+            top = best[here, :]
+            for i in range(len(sides)):
+                sums = scratch[i][1]
+                products = sums[here, :128] + (sums[middle, :128] + sums[middle, 128:]) + sums[after, 128:]
+                score = products * scaled[i][j] - mean * shifted[i][j]
+                partner = masks[i][1][v]
+                counted = partner < total - 128 * j if sides[i][0] else partner >= -128 * j
+                top = jnp.maximum(top, jnp.where(counted, score, -FILL))
+            best[here, :] = top
 
 
 def finish(best, a_ref, out_ref):
@@ -182,10 +190,12 @@
 
 
 def kernel(
-    series, tail, offset, exclusion, out,
+    series_hbm, tail_hbm, offset_hbm, exclusion_hbm, out,
+    series, tail, offset, exclusion,
     ext, x_ref, mean_ref, a_ref, b_ref, w_ref, ones_ref,
-    x_skew, a_skew, b_skew, own_x, own_mean, lhs0, sums0, lhs1, sums1, best,
-    mine, gathered, halo_send, halo_recv, off_send, off_recv,
+    x_skew, a_skew, b_skew, own_x, own_mean,
+    lhs0, sums0, lhs1, sums1, lhs2, sums2, lhs3, sums3, best,
+    mine, gathered, load_sem, halo_send, halo_recv, off_send, off_recv,
     *, n_tm, n_diag, total,
 ):
     tm = lax.axis_index("tm")
@@ -209,14 +219,28 @@
     for k in range(2 * NEAR, 0, -1):
         pl.semaphore_signal(barrier, inc=1, device_id=peer(hop(k)), device_id_type=MESH)
 
+    loads = [
+        pltpu.make_async_copy(source, target, load_sem.at[i])
+        for i, (source, target) in enumerate(
+            ((offset_hbm, offset), (series_hbm, series), (tail_hbm, tail), (exclusion_hbm, exclusion))
+        )
+    ]
+    for load in loads:
+        load.start()
+
+    ext[2 * HALO + SEG :, :] = jnp.zeros((EXT - 2 * HALO - SEG, 128), F32)
+    w_ref[...] = window_weights()
+    ones_ref[...] = w_ref[...].astype(F32)
+    scratch = ((lhs0, sums0), (lhs1, sums1), (lhs2, sums2), (lhs3, sums3))
+    best[...] = jnp.full(best.shape, -FILL, F32)
+
+    edge = has_prev.astype(jnp.int32) + has_next.astype(jnp.int32)
+    for load in loads:
+        load.wait()
+
     mine[0, 0] = offset[0]
     gathered[0, 0] = offset[0]
     ext[HALO : HALO + SEG, :] = series[...]
-    ext[2 * HALO + SEG :, :] = jnp.zeros((EXT - 2 * HALO - SEG, 128), F32)
-    w_ref[...] = window_weights()
-    ones_ref[...] = w_ref[...].astype(F32)
-    scratch = ((lhs0, sums0), (lhs1, sums1))
-    best[...] = jnp.full(best.shape, -FILL, F32)
 
     @pl.when(jnp.logical_not(has_prev))
     def _():
@@ -227,7 +251,6 @@
         ext[HALO + SEG : HALO + SEG + 2, :] = tail[...]
         ext[HALO + SEG + 2 : 2 * HALO + SEG, :] = jnp.zeros((HALO - 2, 128), F32)
 
-    edge = has_prev.astype(jnp.int32) + has_next.astype(jnp.int32)
     pl.semaphore_wait(barrier, 2 * NEAR + edge)
 
     def offset_copy(k):
@@ -280,23 +303,23 @@
     own_rows(mean_ref, own_mean)
     pos0 = (tm * SEG + z * OWN) * 128
 
-    def group(k, carry):
-        @pl.when(k > 2 * NEAR)
-        def _():
-            pltpu.make_async_remote_copy(
-                mine, gathered.at[pl.ds(k, 1)], off_send.at[k], off_recv.at[k],
-                device_id=peer(1), device_id_type=MESH,
-            ).wait_recv()
-
-        first = gathered[k, 0]
+    def pair(t, carry):
+        for i in range(2):
+
+            @pl.when(2 * t + i > 2 * NEAR)
+            def _(k=2 * t + i):
+                pltpu.make_async_remote_copy(
+                    mine, gathered.at[pl.ds(k, 1)], off_send.at[k], off_recv.at[k],
+                    device_id=peer(1), device_id_type=MESH,
+                ).wait_recv()
 
         group_scores(
-            first, exclusion[0], pos0, total,
+            (gathered[2 * t, 0], gathered[2 * t + 1, 0]), exclusion[0], pos0, total,
             x_skew, a_skew, b_skew, own_x, own_mean, ones_ref, scratch, best,
         )
         return carry
 
-    lax.fori_loop(0, n_diag, group, 0)
+    lax.fori_loop(0, n_diag // 2, pair, 0)
     finish(best, a_ref, out)
 
     for k in range(1, n_diag):
@@ -316,16 +339,19 @@
 
     def on_device(series, tail, diag_offsets, exclusion):
         total = series.shape[0] * n_tm
-        vmem = pl.BlockSpec(memory_space=pltpu.VMEM)
-        smem = pl.BlockSpec(memory_space=pltpu.SMEM)
+        anywhere = pl.BlockSpec(memory_space=pltpu.HBM)
         product_rows = KB * (SCORE_BLOCKS + 2)
         side_scratch = [pltpu.VMEM((product_rows, 256), F32)] * 2
         rows = pl.pallas_call(
             functools.partial(kernel, n_tm=n_tm, n_diag=n_diag, total=total),
             out_shape=jax.ShapeDtypeStruct((OWN, 128), F32),
-            in_specs=[vmem, vmem, smem, smem],
-            out_specs=vmem,
+            in_specs=[anywhere] * 4,
+            out_specs=pl.BlockSpec(memory_space=pltpu.VMEM),
             scratch_shapes=[
+                pltpu.VMEM((SEG, 128), F32),
+                pltpu.VMEM((M // 128, 128), F32),
+                pltpu.SMEM((1,), jnp.int32),
+                pltpu.SMEM((1,), jnp.int32),
                 pltpu.VMEM((EXT, 128), F32),
                 pltpu.VMEM((REGION, 128), F32),
                 pltpu.VMEM((REGION, 128), F32),
@@ -338,11 +364,11 @@
                 pltpu.VMEM((8 * SKEWED, 128), F32),
                 pltpu.VMEM((16 * STEPS, 128), F32),
                 pltpu.VMEM((16 * STEPS, 128), F32),
-                *side_scratch,
-                *side_scratch,
+                *side_scratch * 4,
                 pltpu.VMEM((KB * SCORE_BLOCKS, 128), F32),
                 pltpu.SMEM((1, 128), jnp.int32),
                 pltpu.SMEM((16, 128), jnp.int32),
+                pltpu.SemaphoreType.DMA((4,)),
                 pltpu.SemaphoreType.DMA((2,)),
                 pltpu.SemaphoreType.DMA((2,)),
                 pltpu.SemaphoreType.DMA((16,)),

time: 28.3 us -> 26 us (0.919)
  the two profiles are of different devices: /device:TPU:18 before, /device:TPU:10 now
where the time goes in v3:
time: 26 us; the launch traced here: 25.8 us
  Pallas kernels  23.2 us (89%)
  between operations  1.3 us (5%)
  local copies, waits for them, and re-layouts  1.28 us (5%)
    pallas_call x1, Pallas kernels, on_device(): pl.pallas_call(functools.partial(kernel, n_tm=n_tm, n_diag=n_diag, total=...  23.2 us
    unnamed x1, local copies, waits for them, and re-layouts  1.28 us

profile of v3, /device:TPU:10, one launch (start us, length us, event | category | flops | bytes accessed | tf_op | source)
XLA Modules:
  0.0 25.8 jit_solution(10107367172115310371)
XLA Ops:
  1.3 23.2 %profile_rows.1 = f32[8,128]{1,0:T(8,128)} custom-call(f32[128,128]{1,0:T(8,128)} %bitcast.3, f32[2,128]{1,0:T(2,128)} %bitcast.5, s32[1]{0:T(128)S(6)} %copy.6.offset_hbm, s32[1]{0:T(128)S(6)} %copy.7.exclusion_hbm), custom_call_target="tpu_custom_call" | custom-call | tf_op jit(solution)/shard_map/profile_rows/pallas_call | solution.py:345
  24.5 1.3 %copy.8 = f32[1024]{0:T(1024)} copy(f32[1024]{0:T(1024)} %bitcast.4) | data formatting | bytes 8192

commit v4 on v3

--- a/solution.py
+++ b/solution.py
@@ -25,11 +25,9 @@
 EXT = 2 * HALO + SEG + 16
 STEPS = KB // 8
 SCORE_BLOCKS = OWN + 1
-NEAR = 4
-
-
-def hop(k):
-    return (k + 1) // 2 * (1 if k % 2 else -1)
+
+HUBS = 4
+SERVES = ((), (10, 11, 12, 13, 14, 15), (6, 7), (4, 5, 8, 9))
 
 
 def split2(v):
@@ -190,12 +188,12 @@
 
 
 def kernel(
-    series_hbm, tail_hbm, offset_hbm, exclusion_hbm, out,
-    series, tail, offset, exclusion,
+    series_hbm, tail_hbm, offset, exclusion, out,
+    series, tail,
     ext, x_ref, mean_ref, a_ref, b_ref, w_ref, ones_ref,
     x_skew, a_skew, b_skew, own_x, own_mean,
     lhs0, sums0, lhs1, sums1, lhs2, sums2, lhs3, sums3, best,
-    mine, gathered, load_sem, halo_send, halo_recv, off_send, off_recv,
+    mine, table, packed, load_sem, halo_send, halo_recv, row_send, row_recv, reply_send, table_send, table_recv, answer,
     *, n_tm, n_diag, total,
 ):
     tm = lax.axis_index("tm")
@@ -203,64 +201,57 @@
     has_prev = tm > 0
     has_next = tm < n_tm - 1
 
-    def peer(h):
-        return (tm, lax.rem(z + h + n_diag, n_diag))
+    is_hub = z < HUBS
 
     barrier = pltpu.get_barrier_semaphore()
 
-    @pl.when(has_prev)
+    answers = lax.rem(tm, 2) == 1
+
+    @pl.when(jnp.logical_not(answers) & has_prev)
     def _():
         pl.semaphore_signal(barrier, inc=1, device_id=(tm - 1, z), device_id_type=MESH)
 
-    @pl.when(has_next)
+    @pl.when(jnp.logical_not(answers) & has_next)
     def _():
         pl.semaphore_signal(barrier, inc=1, device_id=(tm + 1, z), device_id_type=MESH)
 
-    for k in range(2 * NEAR, 0, -1):
-        pl.semaphore_signal(barrier, inc=1, device_id=peer(hop(k)), device_id_type=MESH)
+    for b in range(n_diag - 1, 0, -1):
+
+        @pl.when(is_hub & (z < b))
+        def _(b=b):
+            pl.semaphore_signal(barrier, inc=1, device_id=(tm, b), device_id_type=MESH)
+
+    mine[0, 0] = offset[0]
+
+    @pl.when(is_hub)
+    def _():
+        table[z, 0] = offset[0]
 
     loads = [
         pltpu.make_async_copy(source, target, load_sem.at[i])
         for i, (source, target) in enumerate(
-            ((offset_hbm, offset), (series_hbm, series), (tail_hbm, tail), (exclusion_hbm, exclusion))
+            ((series_hbm, series), (tail_hbm, tail))
         )
     ]
     for load in loads:
         load.start()
 
-    ext[2 * HALO + SEG :, :] = jnp.zeros((EXT - 2 * HALO - SEG, 128), F32)
-    w_ref[...] = window_weights()
-    ones_ref[...] = w_ref[...].astype(F32)
-    scratch = ((lhs0, sums0), (lhs1, sums1), (lhs2, sums2), (lhs3, sums3))
-    best[...] = jnp.full(best.shape, -FILL, F32)
-
-    edge = has_prev.astype(jnp.int32) + has_next.astype(jnp.int32)
-    for load in loads:
-        load.wait()
-
-    mine[0, 0] = offset[0]
-    gathered[0, 0] = offset[0]
-    ext[HALO : HALO + SEG, :] = series[...]
-
-    @pl.when(jnp.logical_not(has_prev))
-    def _():
-        ext[:HALO, :] = jnp.zeros((HALO, 128), F32)
-
-    @pl.when(jnp.logical_not(has_next))
-    def _():
-        ext[HALO + SEG : HALO + SEG + 2, :] = tail[...]
-        ext[HALO + SEG + 2 : 2 * HALO + SEG, :] = jnp.zeros((HALO - 2, 128), F32)
-
-    pl.semaphore_wait(barrier, 2 * NEAR + edge)
-
-    def offset_copy(k):
-        h = hop(k)
-        near = abs(h) <= NEAR
-        source = mine if near else gathered.at[pl.ds(k - 2 * NEAR, 1)]
-        to = -h if near else (-NEAR if h > 0 else NEAR)
+    def row_copy(to, send_sem):
         return pltpu.make_async_remote_copy(
-            source, gathered.at[pl.ds(k, 1)], off_send.at[k], off_recv.at[k],
-            device_id=peer(to), device_id_type=MESH,
+            mine, table.at[pl.ds(z, 1)], send_sem, row_recv.at[z], device_id=(tm, to), device_id_type=MESH
+        )
+
+    def wait_row(b):
+        pltpu.make_async_remote_copy(
+            mine, table.at[pl.ds(b, 1)], row_send.at[0], row_recv.at[b], device_id=(tm, 0), device_id_type=MESH
+        ).wait_recv()
+
+    half = n_diag // 2
+
+    def table_copy(to, i, part):
+        rows = packed.at[pl.ds(part, 1)]
+        return pltpu.make_async_remote_copy(
+            rows, rows, table_send.at[2 * i + part], table_recv.at[part], device_id=(tm, to), device_id_type=MESH
         )
 
     to_prev = pltpu.make_async_remote_copy(
@@ -272,21 +263,62 @@
         device_id=(tm + 1, z), device_id_type=MESH,
     )
 
-    for k in range(2 * NEAR, 0, -1):
-        offset_copy(k).start()
+    edge = has_prev.astype(jnp.int32) + has_next.astype(jnp.int32)
+    announced = jnp.minimum(z, HUBS) + edge * lax.rem(tm, 2)
+
+    @pl.when(announced > 0)
+    def _():
+        pl.semaphore_wait(barrier, announced)
+
+    @pl.when(answers & has_prev)
+    def _():
+        pl.semaphore_signal(answer.at[1], inc=1, device_id=(tm - 1, z), device_id_type=MESH)
+
+    @pl.when(answers & has_next)
+    def _():
+        pl.semaphore_signal(answer.at[0], inc=1, device_id=(tm + 1, z), device_id_type=MESH)
+
+    for a in range(HUBS):
+
+        @pl.when(z > a)
+        def _(a=a):
+            row_copy(a, row_send.at[a]).start()
+
+    for load in loads:
+        load.wait()
 
     @pl.when(has_prev)
     def _():
+        @pl.when(jnp.logical_not(answers))
+        def _():
+            pl.semaphore_wait(answer.at[0], 1)
+
         to_prev.start()
 
     @pl.when(has_next)
     def _():
+        @pl.when(jnp.logical_not(answers))
+        def _():
+            pl.semaphore_wait(answer.at[1], 1)
+
         to_next.start()
 
-    for k in range(1, 2 * NEAR + 1):
-        offset_copy(k).wait_recv()
-        if k + 2 * NEAR < n_diag:
-            offset_copy(k + 2 * NEAR).start()
+    ext[HALO : HALO + SEG, :] = series[...]
+    ext[2 * HALO + SEG :, :] = jnp.zeros((EXT - 2 * HALO - SEG, 128), F32)
+
+    @pl.when(jnp.logical_not(has_prev))
+    def _():
+        ext[:HALO, :] = jnp.zeros((HALO, 128), F32)
+
+    @pl.when(jnp.logical_not(has_next))
+    def _():
+        ext[HALO + SEG : HALO + SEG + 2, :] = tail[...]
+        ext[HALO + SEG + 2 : 2 * HALO + SEG, :] = jnp.zeros((HALO - 2, 128), F32)
+
+    w_ref[...] = window_weights()
+    ones_ref[...] = w_ref[...].astype(F32)
+    scratch = ((lhs0, sums0), (lhs1, sums1), (lhs2, sums2), (lhs3, sums3))
+    best[...] = jnp.full(best.shape, -FILL, F32)
 
     @pl.when(has_next)
     def _():
@@ -303,18 +335,62 @@
     own_rows(mean_ref, own_mean)
     pos0 = (tm * SEG + z * OWN) * 128
 
+    for b in range(1, HUBS):
+
+        @pl.when(z < b)
+        def _(b=b):
+            wait_row(b)
+            row_copy(b, reply_send.at[b]).start()
+
+    for a in range(HUBS - 1):
+
+        @pl.when(is_hub & (z > a))
+        def _(a=a):
+            wait_row(a)
+
+    @pl.when(is_hub)
+    def _():
+        for b in range(HUBS, half):
+            wait_row(b)
+
+        for b in range(half):
+            packed[0, b] = table[b, 0]
+
+    for hub, served in enumerate(SERVES):
+
+        @pl.when(z == hub)
+        def _(served=served):
+            for i, to in enumerate(served):
+                if to < half:
+                    table_copy(to, i, 0).start()
+
+    @pl.when(jnp.logical_not(is_hub))
+    def _():
+        table_copy(0, 0, 0).wait_recv()
+
     def pair(t, carry):
-        for i in range(2):
-
-            @pl.when(2 * t + i > 2 * NEAR)
-            def _(k=2 * t + i):
-                pltpu.make_async_remote_copy(
-                    mine, gathered.at[pl.ds(k, 1)], off_send.at[k], off_recv.at[k],
-                    device_id=peer(1), device_id_type=MESH,
-                ).wait_recv()
-
+        @pl.when(jnp.logical_not(is_hub) & (t == half // 2))
+        def _():
+            table_copy(0, 0, 1).wait_recv()
+
+        @pl.when(is_hub & (t == half // 2))
+        def _():
+            for b in range(half, n_diag):
+                wait_row(b)
+                packed[1, b - half] = table[b, 0]
+            for hub, served in enumerate(SERVES):
+
+                @pl.when(z == hub)
+                def _(served=served):
+                    for i, to in enumerate(served):
+                        if to >= half:
+                            table_copy(to, i, 0).start()
+                        table_copy(to, i, 1).start()
+
+        part = jnp.where(t < half // 2, 0, 1)
+        column = 2 * t - half * part
         group_scores(
-            (gathered[2 * t, 0], gathered[2 * t + 1, 0]), exclusion[0], pos0, total,
+            (packed[part, column], packed[part, column + 1]), exclusion[0], pos0, total,
             x_skew, a_skew, b_skew, own_x, own_mean, ones_ref, scratch, best,
         )
         return carry
@@ -322,8 +398,25 @@
     lax.fori_loop(0, n_diag // 2, pair, 0)
     finish(best, a_ref, out)
 
-    for k in range(1, n_diag):
-        offset_copy(k).wait_send()
+    for a in range(HUBS):
+
+        @pl.when(z > a)
+        def _(a=a):
+            row_copy(a, row_send.at[a]).wait_send()
+
+    for b in range(1, HUBS):
+
+        @pl.when(z < b)
+        def _(b=b):
+            row_copy(b, reply_send.at[b]).wait_send()
+
+    for hub, served in enumerate(SERVES):
+
+        @pl.when(z == hub)
+        def _(served=served):
+            for i, to in enumerate(served):
+                table_copy(to, i, 0).wait_send()
+                table_copy(to, i, 1).wait_send()
 
     @pl.when(has_prev)
     def _():
@@ -339,19 +432,18 @@
 
     def on_device(series, tail, diag_offsets, exclusion):
         total = series.shape[0] * n_tm
-        anywhere = pl.BlockSpec(memory_space=pltpu.HBM)
+        anywhere = pl.BlockSpec(memory_space=pl.ANY)
+        smem = pl.BlockSpec(memory_space=pltpu.SMEM)
         product_rows = KB * (SCORE_BLOCKS + 2)
         side_scratch = [pltpu.VMEM((product_rows, 256), F32)] * 2
         rows = pl.pallas_call(
             functools.partial(kernel, n_tm=n_tm, n_diag=n_diag, total=total),
             out_shape=jax.ShapeDtypeStruct((OWN, 128), F32),
-            in_specs=[anywhere] * 4,
+            in_specs=[anywhere, anywhere, smem, smem],
             out_specs=pl.BlockSpec(memory_space=pltpu.VMEM),
             scratch_shapes=[
                 pltpu.VMEM((SEG, 128), F32),
                 pltpu.VMEM((M // 128, 128), F32),
-                pltpu.SMEM((1,), jnp.int32),
-                pltpu.SMEM((1,), jnp.int32),
                 pltpu.VMEM((EXT, 128), F32),
                 pltpu.VMEM((REGION, 128), F32),
                 pltpu.VMEM((REGION, 128), F32),
@@ -368,11 +460,16 @@
                 pltpu.VMEM((KB * SCORE_BLOCKS, 128), F32),
                 pltpu.SMEM((1, 128), jnp.int32),
                 pltpu.SMEM((16, 128), jnp.int32),
-                pltpu.SemaphoreType.DMA((4,)),
+                pltpu.SMEM((2, 128), jnp.int32),
                 pltpu.SemaphoreType.DMA((2,)),
                 pltpu.SemaphoreType.DMA((2,)),
+                pltpu.SemaphoreType.DMA((2,)),
+                pltpu.SemaphoreType.DMA((HUBS,)),
                 pltpu.SemaphoreType.DMA((16,)),
-                pltpu.SemaphoreType.DMA((16,)),
+                pltpu.SemaphoreType.DMA((HUBS,)),
+                pltpu.SemaphoreType.DMA((2 * max(map(len, SERVES)),)),
+                pltpu.SemaphoreType.DMA((2,)),
+                pltpu.SemaphoreType.REGULAR((2,)),
             ],
             compiler_params=pltpu.CompilerParams(collective_id=0, has_side_effects=True),
             name="profile_rows",

time: 26 us -> 24.3 us (0.935)
  the two profiles are of different devices: /device:TPU:10 before, /device:TPU:320 now
where the time goes in v4:
time: 24.3 us; the launch traced here: 24.1 us
  Pallas kernels  21.5 us (88%)
  between operations  1.3 us (5%)
  local copies, waits for them, and re-layouts  1.28 us (5%)
    pallas_call x1, Pallas kernels, on_device(): pl.pallas_call(functools.partial(kernel, n_tm=n_tm, n_diag=n_diag, total=...  21.5 us
    unnamed x1, local copies, waits for them, and re-layouts  1.28 us

profile of v4, /device:TPU:320, one launch (start us, length us, event | category | flops | bytes accessed | tf_op | source)
XLA Modules:
  0.0 24.1 jit_solution(11835482967758340383)
XLA Ops:
  1.3 21.5 %profile_rows.1 = f32[8,128]{1,0:T(8,128)} custom-call(f32[128,128]{1,0:T(8,128)} %bitcast.3, f32[2,128]{1,0:T(2,128)} %bitcast.5, s32[1]{0:T(128)S(6)} %copy.6.offset, s32[1]{0:T(128)S(6)} %copy.7.exclusion), custom_call_target="tpu_custom_call" | custom-call | tf_op jit(solution)/shard_map/profile_rows/pallas_call | solution.py:439
  22.8 1.3 %copy.8 = f32[1024]{0:T(1024)} copy(f32[1024]{0:T(1024)} %bitcast.4) | data formatting | bytes 8192

commit v5 on v4

--- a/solution.py
+++ b/solution.py
@@ -27,7 +27,7 @@
 SCORE_BLOCKS = OWN + 1
 
 HUBS = 4
-SERVES = ((), (10, 11, 12, 13, 14, 15), (6, 7), (4, 5, 8, 9))
+SERVES = ((), (0, 10, 11, 12, 13, 14, 15), (6, 7), (4, 5, 8, 9))
 
 
 def split2(v):
@@ -201,7 +201,9 @@
     has_prev = tm > 0
     has_next = tm < n_tm - 1
 
-    is_hub = z < HUBS
+    late = tm == 0
+    is_hub = (z < HUBS) & jnp.logical_not(late & (z == 0))
+    served_zero = late & (z == 0)
 
     barrier = pltpu.get_barrier_semaphore()
 
@@ -220,6 +222,10 @@
         @pl.when(is_hub & (z < b))
         def _(b=b):
             pl.semaphore_signal(barrier, inc=1, device_id=(tm, b), device_id_type=MESH)
+
+    @pl.when(is_hub & late)
+    def _():
+        pl.semaphore_signal(barrier, inc=1, device_id=(tm, 0), device_id_type=MESH)
 
     mine[0, 0] = offset[0]
 
@@ -246,6 +252,9 @@
             mine, table.at[pl.ds(b, 1)], row_send.at[0], row_recv.at[b], device_id=(tm, 0), device_id_type=MESH
         ).wait_recv()
 
+    def sends_to(a):
+        return (z > a) & jnp.logical_not(late) if a == 0 else (z > a) | served_zero
+
     half = n_diag // 2
 
     def table_copy(to, i, part):
@@ -264,7 +273,8 @@
     )
 
     edge = has_prev.astype(jnp.int32) + has_next.astype(jnp.int32)
-    announced = jnp.minimum(z, HUBS) + edge * lax.rem(tm, 2)
+    hubs_below = jnp.where(served_zero, HUBS - 1, jnp.minimum(z, HUBS) - (late & (z > 0)).astype(jnp.int32))
+    announced = hubs_below + edge * lax.rem(tm, 2)
 
     @pl.when(announced > 0)
     def _():
@@ -280,7 +290,7 @@
 
     for a in range(HUBS):
 
-        @pl.when(z > a)
+        @pl.when(sends_to(a))
         def _(a=a):
             row_copy(a, row_send.at[a]).start()
 
@@ -337,7 +347,7 @@
 
     for b in range(1, HUBS):
 
-        @pl.when(z < b)
+        @pl.when(is_hub & (z < b))
         def _(b=b):
             wait_row(b)
             row_copy(b, reply_send.at[b]).start()
@@ -362,7 +372,10 @@
         def _(served=served):
             for i, to in enumerate(served):
                 if to < half:
-                    table_copy(to, i, 0).start()
+
+                    @pl.when(late | (to > 0))
+                    def _(i=i, to=to):
+                        table_copy(to, i, 0).start()
 
     @pl.when(jnp.logical_not(is_hub))
     def _():
@@ -373,22 +386,38 @@
         def _():
             table_copy(0, 0, 1).wait_recv()
 
-        @pl.when(is_hub & (t == half // 2))
-        def _():
-            for b in range(half, n_diag):
-                wait_row(b)
-                packed[1, b - half] = table[b, 0]
-            for hub, served in enumerate(SERVES):
-
-                @pl.when(z == hub)
-                def _(served=served):
-                    for i, to in enumerate(served):
-                        if to >= half:
-                            table_copy(to, i, 0).start()
+        def take_row(b):
+            wait_row(b)
+            packed[1, b - half] = table[b, 0]
+
+        for hub, served in enumerate(SERVES):
+            if not served:
+                for q in range(half // 2):
+
+                    @pl.when(is_hub & (z == hub) & (t == half // 2 + q))
+                    def _(q=q):
+                        take_row(n_diag - 1 - 2 * q)
+                        take_row(n_diag - 2 - 2 * q)
+
+                continue
+
+            @pl.when((z == hub) & (t == half // 2))
+            def _(served=served):
+                for i, to in enumerate(served):
+                    if to >= half:
+                        take_row(to)
+                        table_copy(to, i, 0).start()
+                for b in range(half, n_diag):
+                    if b not in served:
+                        take_row(b)
+                for i, to in enumerate(served):
+
+                    @pl.when(late | (to > 0))
+                    def _(i=i, to=to):
                         table_copy(to, i, 1).start()
 
         part = jnp.where(t < half // 2, 0, 1)
-        column = 2 * t - half * part
+        column = jnp.where(t < half // 2, 2 * t, 2 * (n_diag - half // 2 - 1 - t - half // 2))
         group_scores(
             (packed[part, column], packed[part, column + 1]), exclusion[0], pos0, total,
             x_skew, a_skew, b_skew, own_x, own_mean, ones_ref, scratch, best,
@@ -400,13 +429,13 @@
 
     for a in range(HUBS):
 
-        @pl.when(z > a)
+        @pl.when(sends_to(a))
         def _(a=a):
             row_copy(a, row_send.at[a]).wait_send()
 
     for b in range(1, HUBS):
 
-        @pl.when(z < b)
+        @pl.when(is_hub & (z < b))
         def _(b=b):
             row_copy(b, reply_send.at[b]).wait_send()
 
@@ -415,8 +444,11 @@
         @pl.when(z == hub)
         def _(served=served):
             for i, to in enumerate(served):
-                table_copy(to, i, 0).wait_send()
-                table_copy(to, i, 1).wait_send()
+
+                @pl.when(late | (to > 0))
+                def _(i=i, to=to):
+                    table_copy(to, i, 0).wait_send()
+                    table_copy(to, i, 1).wait_send()
 
     @pl.when(has_prev)
     def _():

time: 24.3 us -> 22.8 us (0.938)
  the two profiles are of different devices: /device:TPU:320 before, /device:TPU:1 now
where the time goes in v5:
time: 22.8 us; the launch traced here: 22.6 us
  Pallas kernels  20.1 us (88%)
  between operations  1.3 us (6%)
  local copies, waits for them, and re-layouts  1.28 us (6%)
    pallas_call x1, Pallas kernels, on_device(): pl.pallas_call(functools.partial(kernel, n_tm=n_tm, n_diag=n_diag, total=...  20.1 us
    unnamed x1, local copies, waits for them, and re-layouts  1.28 us

profile of v5, /device:TPU:1, one launch (start us, length us, event | category | flops | bytes accessed | tf_op | source)
XLA Modules:
  0.0 22.6 jit_solution(7699741738570088100)
XLA Ops:
  1.3 20.1 %profile_rows.1 = f32[8,128]{1,0:T(8,128)} custom-call(f32[128,128]{1,0:T(8,128)} %bitcast.3, f32[2,128]{1,0:T(2,128)} %bitcast.5, s32[1]{0:T(128)S(6)} %copy.6.offset, s32[1]{0:T(128)S(6)} %copy.7.exclusion), custom_call_target="tpu_custom_call" | custom-call | tf_op jit(solution)/shard_map/profile_rows/pallas_call | solution.py:471
  21.4 1.3 %copy.8 = f32[1024]{0:T(1024)} copy(f32[1024]{0:T(1024)} %bitcast.4) | data formatting | bytes 8192

commit v6 on v5

--- a/solution.py
+++ b/solution.py
@@ -470,7 +470,7 @@
         side_scratch = [pltpu.VMEM((product_rows, 256), F32)] * 2
         rows = pl.pallas_call(
             functools.partial(kernel, n_tm=n_tm, n_diag=n_diag, total=total),
-            out_shape=jax.ShapeDtypeStruct((OWN, 128), F32),
+            out_shape=pltpu.VMEM((OWN, 128), F32),
             in_specs=[anywhere, anywhere, smem, smem],
             out_specs=pl.BlockSpec(memory_space=pltpu.VMEM),
             scratch_shapes=[

time: 22.8 us -> 21.5 us (0.943)
  local copies, waits for them, and re-layouts: 1.28 us -> 0.6 us
  Pallas kernels: 20.1 us -> 19.5 us
    unnamed x1, local copies, waits for them, and re-layouts: 1.28 us -> 0.6 us
    pallas_call x1, Pallas kernels: 20.1 us -> 19.5 us  [on_device(): pl.pallas_call(functools.partial(kernel, n_tm=n_tm, n_diag=n_diag, total=...]
where the time goes in v6:
time: 21.5 us; the launch traced here: 21.4 us
  Pallas kernels  19.5 us (91%)
  between operations  1.3 us (6%)
  local copies, waits for them, and re-layouts  0.6 us (3%)
    pallas_call x1, Pallas kernels, on_device(): pl.pallas_call(functools.partial(kernel, n_tm=n_tm, n_diag=n_diag, total=...  19.5 us
    unnamed x1, local copies, waits for them, and re-layouts  0.6 us

profile of v6, /device:TPU:1, one launch (start us, length us, event | category | flops | bytes accessed | tf_op | source)
XLA Modules:
  0.0 21.4 jit_solution(2587378265690586728)
XLA Ops:
  1.3 19.5 %profile_rows.1 = f32[8,128]{1,0:T(8,128)S(1)} custom-call(f32[128,128]{1,0:T(8,128)} %bitcast.4, f32[2,128]{1,0:T(2,128)} %bitcast.5, s32[1]{0:T(128)S(6)} %copy.7.offset, s32[1]{0:T(128)S(6)} %copy.8.exclusion), custom_call_target="tpu_custom_call" | custom-call | tf_op jit(solution)/shard_map/profile_rows/pallas_call | solution.py:471
  20.8 0.6 %copy.6 = f32[1024]{0:T(1024)} copy(f32[1024]{0:T(1024)S(1)} %bitcast.3) | data formatting | bytes 8192

commit v7 on v6

--- a/solution.py
+++ b/solution.py
@@ -217,11 +217,13 @@
     def _():
         pl.semaphore_signal(barrier, inc=1, device_id=(tm + 1, z), device_id_type=MESH)
 
-    for b in range(n_diag - 1, 0, -1):
-
-        @pl.when(is_hub & (z < b))
-        def _(b=b):
-            pl.semaphore_signal(barrier, inc=1, device_id=(tm, b), device_id_type=MESH)
+    @pl.when(is_hub)
+    def _():
+        for b in range(n_diag - 1, 0, -1):
+
+            @pl.when(z < b)
+            def _(b=b):
+                pl.semaphore_signal(barrier, inc=1, device_id=(tm, b), device_id_type=MESH)
 
     @pl.when(is_hub & late)
     def _():

time: 21.5 us -> 21.6 us (level)
  no operation moved by 1% of the time
where the time goes in v7:
time: 21.6 us; the launch traced here: 21.4 us
  Pallas kernels  19.5 us (90%)
  between operations  1.3 us (6%)
  local copies, waits for them, and re-layouts  0.6 us (3%)
    pallas_call x1, Pallas kernels, on_device(): pl.pallas_call(functools.partial(kernel, n_tm=n_tm, n_diag=n_diag, total=...  19.5 us
    unnamed x1, local copies, waits for them, and re-layouts  0.6 us

profile of v7, /device:TPU:1, one launch (start us, length us, event | category | flops | bytes accessed | tf_op | source)
XLA Modules:
  0.0 21.4 jit_solution(15964309744066091308)
XLA Ops:
  1.3 19.5 %profile_rows.1 = f32[8,128]{1,0:T(8,128)S(1)} custom-call(f32[128,128]{1,0:T(8,128)} %bitcast.4, f32[2,128]{1,0:T(2,128)} %bitcast.5, s32[1]{0:T(128)S(6)} %copy.7.offset, s32[1]{0:T(128)S(6)} %copy.8.exclusion), custom_call_target="tpu_custom_call" | custom-call | tf_op jit(solution)/shard_map/profile_rows/pallas_call | solution.py:473
  20.8 0.6 %copy.6 = f32[1024]{0:T(1024)} copy(f32[1024]{0:T(1024)S(1)} %bitcast.3) | data formatting | bytes 8192
